TPU v7x, 32 devices: a whole 2x2x4 slice. The times are simulated.
32 devices in a mesh: pts: 32 (over z, y, x, core).
Axes of the slice: x: 2, y: 2, z: 4, core: 2. Of those that a mesh axis runs over, the one named last changes fastest.
Arguments:
- point_data: float32 [5, 32768], P(None, 'pts'), may hold values from -1 to 1
- point_counts: int32 [32], P('pts'), may hold values from 64 to 1024, as said below
- point_offsets: int32 [32], P('pts'), may hold values from 0 to 960, as said below
- in_weight: float32 [3, 256], replicated, may hold values from -6 to 6
- input_bias: float32 [256], replicated, may hold values from -3 to 3
- hidden_layer_weight: float32 [3, 256, 256], replicated, may hold values from -0.5 to 0.5
- hidden_bias: float32 [3, 256], replicated, may hold values from -3 to 3
- output_weight: float32 [3, 256], replicated, may hold values from -0.75 to 0.75
- out_bias: float32 [3], replicated, may hold values from -3 to 3
Outputs:
- grad_in_weight: float32 [3, 256], replicated
- grad_in_bias: float32 [256], replicated
- grad_hidden_weight: float32 [3, 256, 256], replicated
- grad_hidden_bias: float32 [3, 256], replicated
- grad_out_weight: float32 [3, 256], replicated
- grad_out_bias: float32 [3], replicated
- term_means: float32 [3], replicated
Inputs may be any that keep to these rules, and one draw needn't show every extreme that they name: `point_counts`: some device has exactly 1024 live points and another exactly 64. A device's live points fill its slots point_offsets to point_offsets + point_counts - 1, all within its 1024 slots.
All inputs are finite; a program needn't handle non-finite values.
Results may differ from a plain program's by a relative error of at most 0.0001.
Values sent between devices are 32-bit elements; how exact they have to be, the bound alone decides.
A program may use at most 64 MiB of HBM per device.

v0:
```python
import functools

import jax
import jax.numpy as jnp
from jax import lax
from jax.experimental import pallas as pl
from jax.experimental.pallas import tpu as pltpu
from jax.sharding import PartitionSpec as P

viscosity = 0.2
term_weights = (2.0, 1.0, 1.0)
twice = 2.0 * viscosity
B = 256
R = 16

bf16, f32 = jnp.bfloat16, jnp.float32


def split(x):
    hi = x.astype(bf16)
    return hi, (x - hi.astype(f32)).astype(bf16)


def nn(a, b):
    return lax.dot_general(a, b, (((1,), (0,)), ((), ())), preferred_element_type=f32)


def nt(a, b):
    return lax.dot_general(a, b, (((1,), (1,)), ((), ())), preferred_element_type=f32)


def row_sums(x):
    ones = jnp.ones((8, x.shape[1]), f32)
    return lax.dot_general(
        ones,
        x,
        (((1,), (1,)), ((), ())),
        precision=lax.Precision.HIGHEST,
        preferred_element_type=f32,
    )


def local_kernel(
    width,
    hid,
    count_ref,
    offset_ref,
    data_ref,
    in_ref,
    inb_ref,
    w_ref,
    hb_ref,
    wo_ref,
    bo_ref,
    out_ref,
    wcat,
    wtcat,
    wocat,
    wotcat,
    cols,
    z_ref,
    a_ref,
    dz_ref,
    da_ref,
    dout_ref,
    vec,
    tall,
):
    H = width
    for l in range(hid):
        hi, lo = split(w_ref[l])
        wcat[l, :, 0:H] = hi
        wcat[l, :, H : 2 * H] = lo
        wcat[l, :, 2 * H : 3 * H] = hi
        hi, lo = split(w_ref[l].T)
        wtcat[l, :, 0:H] = hi
        wtcat[l, :, H : 2 * H] = lo
        wtcat[l, :, 2 * H : 3 * H] = hi
    tall[...] = jnp.zeros_like(tall)
    tall[0:3, :] = in_ref[...]
    tall[3:4, :] = inb_ref[...]
    tall[4 : 4 + hid, :] = hb_ref[...]
    cols[...] = tall[...].T
    tall[...] = jnp.zeros_like(tall)
    tall[0:3, :] = wo_ref[...]
    hi, lo = split(tall[0:16, :])
    wocat[:, 0:H] = hi
    wocat[:, H : 2 * H] = lo
    wocat[:, 2 * H : 3 * H] = hi
    tall[0:16, :] = hi.astype(f32)
    tall[16:32, :] = lo.astype(f32)
    tall[32:48, :] = hi.astype(f32)
    wotcat[...] = tall[...].T.astype(bf16)
    tall[...] = jnp.zeros_like(tall)
    vec[...] = jnp.zeros_like(vec)
    out_ref[...] = jnp.zeros_like(out_ref)
    dout_ref[...] = jnp.zeros_like(dout_ref)

    count = count_ref[0]
    start = offset_ref[0]
    first = start // B
    end = (start + count + B - 1) // B

    def put_jets(ref, rows, jets, l=None):
        for j, v in enumerate(jets):
            hi, lo = split(v)
            lanes = slice(j * B, (j + 1) * B)
            for k, part in enumerate((hi, hi, lo)):
                at = slice(k * H + rows, k * H + rows + R)
                if l is None:
                    ref[at, lanes] = part
                else:
                    ref[l, at, lanes] = part

    def column(k, rows):
        return jnp.broadcast_to(cols[rows : rows + R, k : k + 1], (R, B))

    def tanh_jets(a, zx, zy, zt):
        s = 1.0 - a * a
        q = zx * zx + zy * zy
        return a, s * zx, s * zy, s * (zt + (twice * a) * q)

    def half(v):
        return v[:, 0 : B // 2] + v[:, B // 2 : B]

    def tanh_back(a, zx, zy, zt, da, dax, day, dat):
        s = 1.0 - a * a
        q = zx * zx + zy * zy
        ca = twice * a
        ds = dax * zx + day * zy + dat * (zt + ca * q)
        dz = s * (da + (twice * dat) * (s * q) - 2.0 * (a * ds))
        e = 2.0 * (ca * dat)
        return dz, s * (dax + e * zx), s * (day + e * zy), s * dat

    def step(index, carry):
        lanes = pl.ds(pl.multiple_of(index * B, B), B)
        x = data_ref[0:1, lanes]
        y = data_ref[1:2, lanes]
        t = data_ref[2:3, lanes]
        fx = data_ref[3:4, lanes]
        fy = data_ref[4:5, lanes]
        slots = index * B + lax.broadcasted_iota(jnp.int32, (1, B), 1)
        mask = ((slots >= start) & (slots < start + count)).astype(f32)
        for r in range(0, H, R):
            wx, wy, wt = column(0, r), column(1, r), column(2, r)
            a = jnp.tanh(wx * x + wy * y + wt * t + column(3, r))
            z_ref[0, r : r + R, 0:B] = a
            put_jets(a_ref, r, tanh_jets(a, wx, wy, wt), 0)
        for l in range(hid):
            z_ref[l + 1] = nn(wcat[l], a_ref[l])
            for r in range(0, H, R):
                rows = slice(r, r + R)
                a = jnp.tanh(z_ref[l + 1, rows, 0:B] + column(4 + l, r))
                z_ref[l + 1, rows, 0:B] = a
                zx, zy, zt = (z_ref[l + 1, rows, j * B : (j + 1) * B] for j in (1, 2, 3))
                put_jets(a_ref, r, tanh_jets(a, zx, zy, zt), l + 1)
        out = nn(wocat[...], a_ref[hid])
        u = out[0:1, 0:B] + bo_ref[0]
        v = out[1:2, 0:B] + bo_ref[1]
        ux, vx, px = (out[k : k + 1, B : 2 * B] for k in range(3))
        uy, vy, py = (out[k : k + 1, 2 * B : 3 * B] for k in range(3))
        ut, vt = (out[k : k + 1, 3 * B : 4 * B] for k in range(2))
        c = mask * (ux + vy)
        mx = mask * (ut + u * ux + v * uy + px - fx)
        my = mask * (vt + u * vx + v * vy + py - fy)
        rc = (2.0 * term_weights[0]) * c
        rx = (2.0 * term_weights[1]) * mx
        ry = (2.0 * term_weights[2]) * my
        du = rx * ux + ry * vx
        dv = rx * uy + ry * vy
        row = lax.broadcasted_iota(jnp.int32, (R, B), 0)
        zero = jnp.zeros((1, B), f32)

        def three(p0, p1, p2):
            return jnp.where(
                row == 0, p0, jnp.where(row == 1, p1, jnp.where(row == 2, p2, 0.0))
            )

        tall[0:16, :] += jnp.where(row < 3, three(c * c, mx * mx, my * my), 0.0) + jnp.where(
            row == 3, du, jnp.where(row == 4, dv, 0.0)
        )
        douts = (
            three(du, dv, zero),
            three(rc + rx * u, ry * u, rx),
            three(rx * v, rc + ry * v, ry),
            three(rx, ry, zero),
        )
        for j, d in enumerate(douts):
            hi, lo = split(d)
            at = slice(j * B, (j + 1) * B)
            dout_ref[0:16, at] = hi
            dout_ref[16:32, at] = hi
            dout_ref[32:48, at] = lo
        both = nt(dout_ref[16:48, :], a_ref[hid, 0:H, :])
        both = both[0:16] + both[16:32] + nt(dout_ref[0:16, :], a_ref[hid, 2 * H : 3 * H, :])
        out_ref[hid * H + 8 : hid * H + 16, :] += both[0:8]
        da_ref[...] = nn(wotcat[...], dout_ref[...])
        for l in range(hid, 0, -1):
            for r in range(0, H, R):
                rows = slice(r, r + R)
                a, zx, zy, zt = (z_ref[l, rows, j * B : (j + 1) * B] for j in range(4))
                ds = (da_ref[rows, j * B : (j + 1) * B] for j in range(4))
                dz = tanh_back(a, zx, zy, zt, *ds)
                put_jets(dz_ref, r, dz)
                vec[3 + l, rows, :] += half(dz[0])
            da_ref[...] = nn(wtcat[l - 1], dz_ref[...])
            both = nt(dz_ref[H : 3 * H, :], a_ref[l - 1, 0:H, :])
            both = both[0:H] + both[H : 2 * H]
            both = both + nt(dz_ref[0:H, :], a_ref[l - 1, 2 * H : 3 * H, :])
            out_ref[(l - 1) * H : l * H, :] += both
        for r in range(0, H, R):
            rows = slice(r, r + R)
            a = z_ref[0, rows, 0:B]
            ds = (da_ref[rows, j * B : (j + 1) * B] for j in range(4))
            dz, dzx, dzy, dzt = tanh_back(a, column(0, r), column(1, r), column(2, r), *ds)
            vec[0, rows, :] += half(dz * x + dzx)
            vec[1, rows, :] += half(dz * y + dzy)
            vec[2, rows, :] += half(dz * t + dzt)
            vec[3, rows, :] += half(dz)
        return carry

    lax.fori_loop(first, end, step, 0)
    base = hid * H
    for k in range(4 + hid):
        out_ref[base + k : base + k + 1, :] = row_sums(vec[k])[0:1]
    lane = lax.broadcasted_iota(jnp.int32, (1, tall.shape[0]), 1)
    scalars = row_sums(tall[...])[0:1] + jnp.where(lane == 6, count.astype(f32), 0.0)
    out_ref[base + 7 : base + 8, 0 : tall.shape[0]] = scalars


def local_terms(counts, offsets, data, in_w, in_b, w, hb, wo, bo):
    hid, H, _ = w.shape
    vm = pl.BlockSpec(memory_space=pltpu.VMEM)
    sm = pl.BlockSpec(memory_space=pltpu.SMEM)
    return pl.pallas_call(
        functools.partial(local_kernel, H, hid),
        out_shape=jax.ShapeDtypeStruct((hid * H + 16, H), f32),
        in_specs=[sm, sm, vm, vm, vm, vm, vm, vm, sm],
        out_specs=vm,
        scratch_shapes=[
            pltpu.VMEM((hid, H, 3 * H), bf16),
            pltpu.VMEM((hid, H, 3 * H), bf16),
            pltpu.VMEM((16, 3 * H), bf16),
            pltpu.VMEM((H, 128), bf16),
            pltpu.VMEM((H, 128), f32),
            pltpu.VMEM((hid + 1, H, 4 * B), f32),
            pltpu.VMEM((hid + 1, 3 * H, 4 * B), bf16),
            pltpu.VMEM((3 * H, 4 * B), bf16),
            pltpu.VMEM((H, 4 * B), f32),
            pltpu.VMEM((128, 4 * B), bf16),
            pltpu.VMEM((4 + hid, H, 128), f32),
            pltpu.VMEM((128, H), f32),
        ],
        compiler_params=pltpu.CompilerParams(vmem_limit_bytes=56 * 1024 * 1024),
        name="local_terms",
    )(counts, offsets, data, in_w, in_b.reshape(1, H), w, hb, wo, bo)


def shards(counts_data, counts, offsets, in_w, in_b, w, hb, wo, bo):
    hid, H, _ = w.shape
    mine = local_terms(counts, offsets, counts_data, in_w, in_b, w, hb, wo, bo)
    g = lax.psum(mine, "pts")
    base = hid * H
    total = g[base + 7, 6]
    g = g / total
    return (
        g[base : base + 3],
        g[base + 3],
        g[:base].reshape(hid, H, H),
        g[base + 4 : base + 4 + hid],
        g[base + 8 : base + 11],
        g[base + 7, 3:6],
        g[base + 7, 0:3],
    )


def solution(mesh):
    placed = (P(None, "pts"), P("pts"), P("pts"), P(), P(), P(), P(), P(), P())
    return jax.shard_map(
        shards,
        mesh=mesh,
        in_specs=placed,
        out_specs=(P(), P(), P(), P(), P(), P(), P()),
        check_vma=False,
    )
```

profile of v0, /device:TPU:0, one launch (start us, length us, event | category | flops | bytes accessed | tf_op | source)
XLA Modules:
  0.0 179.0 jit_solution(11603365515365797958)
XLA Ops:
  7.2 0.0 all-reduce.2.cloned.1.call-start
  8.5 20.8 %local_terms.1 = f32[784,256]{1,0:T(8,128)} custom-call(s32[1]{0:T(128)S(6)} %copy.17.count_ref, s32[1]{0:T(128)S(6)} %copy.18.offset_ref, f32[5,1024]{1,0:T(8,128)} %data_ref.1, f32[3,256]{1,0:T(4,128)} %in_ref.1, f32[1,256]{1,0:T(1,128)} %bitcast.9, f32[3,256,256]{2,1,0:T(8,128)} %w_ref.1, f32[3,256]{1,0:T(4,128)} %hb_ref.1, f32[3,256]{1,0:T(4,128)} %wo_ref.1, ...), custom_call_target="tpu_custom_call" | custom-call | tf_op jit(solution)/shard_map/local_terms/pallas_call | solution.py:235
  29.3 0.0 all-reduce.2.cloned.1.call-update
  29.4 137.0 %all-reduce.2.cloned.1.call-done = f32[784,256]{1,0:T(8,128)} async-done(((f32[784,256]{1,0:T(8,128)}), f32[784,256]{1,0:T(8,128)}) %all-reduce.2.cloned.1.call-update) | async-done | bytes 802832 | tf_op jit(solution)/shard_map/psum | solution.py:262
  166.4 1.3 slice.32
  167.7 1.8 %broadcast_divide_fusion = f32[784,256]{1,0:T(8,128)S(1)} fusion(f32[784,256]{1,0:T(8,128)} %all-reduce.2.cloned.1.call-done, f32[]{:T(128)} %bitcast.1), kind=kLoop, calls=%fused_computation | loop fusion | flops 200704 | bytes 1605636 | tf_op jit(solution)/shard_map/div | solution.py:265
  169.5 0.6 slice.34
  170.1 0.6 slice_bitcast_fusion
  170.7 0.6 fusion
  171.3 0.9 slice.35
Async XLA Ops:
  7.2 159.2 %all-reduce.2.cloned.1.call-start = ((), (), s32[]{:S(2)}) async-start(), calls=%async_computation | async-start | bytes 1605632 | tf_op jit(solution)/shard_map/psum | solution.py:262
Sparse Core Ops, SparseCore 0:
  29.5 136.8 all-reduce.1
where the time goes:
time: 179 us
  waiting for transfers between devices  137 us (77%)
  Pallas kernels  20.8 us (12%)
  between operations  15.3 us (9%)
  local copies, waits for them, and re-layouts  3.93 us (2%)
  other arithmetic  1.84 us (1%)
    psum x1, waiting for transfers between devices, shards(): g = lax.psum(mine, 'pts')  137 us
    pallas_call x1, Pallas kernels, local_terms(): pl.pallas_call(functools.partial(local_kernel, H, hid), out_shape=jax.Sha...  20.8 us
  transfers between devices with their start and end apart: 1, of which 1 were waited for; matrix products, arithmetic and copies ran while one was open for 0% of the time, Pallas kernels for 0%

commit v1 on v0

--- a/solution.py
+++ b/solution.py
@@ -256,28 +256,170 @@
     )(counts, offsets, data, in_w, in_b.reshape(1, H), w, hb, wo, bo)
 
 
-def shards(counts_data, counts, offsets, in_w, in_b, w, hb, wo, bo):
+MESH = pl.DeviceIdType.MESH
+
+def stages_of(n, rows):
+    out, stride = [], 1
+    radices = []
+    left = n
+    if left % 2 == 0:
+        radices.append(2); left //= 2
+    while left % 4 == 0:
+        radices.append(4); left //= 4
+    if left > 1:
+        radices.append(left)
+    for r in radices:
+        scatter = rows % (8 * r) == 0
+        if scatter:
+            rows //= r
+        out.append((stride, r, rows, scatter))
+        stride *= r
+    return out
+
+def ar_kernel(n, hid, H, stages, order, x_ref, w_ref, gi_ref, gb_ref, gh_ref, go_ref, gob_ref, terms_ref, *scratch):
+    ns = len(stages)
+    bufs = scratch[:ns]
+    accs = scratch[ns:2 * ns]
+    sbufs = scratch[2 * ns:3 * ns]
+    saccs = scratch[3 * ns]
+    send, recv, gsend, grecv, ssend, srecv = scratch[3 * ns + 1:]
+    me = lax.axis_index("pts")
+    peers, digit = [], []
+    for stride, r, rows, sc in stages:
+        d = (me // stride) % r
+        digit.append(d)
+        peers.append([me + ((d + k) % r - d) * stride for k in range(1, r)])
+    barrier = pltpu.get_barrier_semaphore()
+    cnt = 0
+    for ps in peers:
+        for p in ps:
+            pl.semaphore_signal(barrier, inc=1, device_id=(p,), device_id_type=MESH)
+            cnt += 1
+    pl.semaphore_wait(barrier, cnt)
+    hid_rows = hid * H
+
+    def small_src(s):
+        return x_ref.at[hid_rows:hid_rows + 16, :] if s == 0 else saccs.at[s - 1]
+
+    def small_start(s):
+        cs = []
+        for k, p in enumerate(peers[s]):
+            c = pltpu.make_async_remote_copy(small_src(s), sbufs[s].at[k], ssend.at[s, k], srecv.at[s, k], device_id=(p,), device_id_type=MESH)
+            c.start(); cs.append(c)
+        return cs
+
+    def small_finish(s, cs):
+        for c in cs:
+            c.wait()
+        v = small_src(s)[...]
+        for k in range(len(cs)):
+            v = v + sbufs[s][k]
+        saccs[s] = v
+
+    def src_rows(l, s, at, rows):
+        if s == 0:
+            return x_ref.at[pl.ds(pl.multiple_of(l * H + at, 8), rows), :]
+        return accs[s - 1].at[l, pl.ds(pl.multiple_of(at, 8), rows), :]
+
+    def start(l, s):
+        stride, r, rows, sc = stages[s]
+        cs = []
+        for k, p in enumerate(peers[s]):
+            at = ((digit[s] + k + 1) % r) * rows if sc else 0
+            c = pltpu.make_async_remote_copy(src_rows(l, s, at, rows), bufs[s].at[l, k], send.at[l, s, k], recv.at[l, s, k], device_id=(p,), device_id_type=MESH)
+            c.start(); cs.append(c)
+        return cs
+
+    def finish(l, s, cs, scale=None):
+        stride, r, rows, sc = stages[s]
+        for c in cs:
+            c.wait()
+        v = src_rows(l, s, digit[s] * rows if sc else 0, rows)[...]
+        for k in range(r - 1):
+            v = v + bufs[s][l, k]
+        if scale is not None:
+            w_ref[l, pl.ds(pl.multiple_of(base[s], 8), rows), :] = v * scale
+        else:
+            accs[s][l] = v
+
+    base, b = [], 0
+    for s, (stride, r, rows, sc) in enumerate(stages):
+        if sc:
+            b = b + digit[s] * rows
+        base.append(b)
+
+    def gstart(l, s):
+        stride, r, rows, sc = stages[s]
+        if not sc:
+            return []
+        at = pl.ds(pl.multiple_of(base[s], 8), rows)
+        cs = []
+        for k, p in enumerate(peers[s]):
+            c = pltpu.make_async_remote_copy(w_ref.at[l, at, :], w_ref.at[l, at, :], gsend.at[l, s, k], grecv.at[l, s, k], device_id=(p,), device_id_type=MESH)
+            c.start(); cs.append(c)
+        return cs
+
+    flight = {}
+    sf = small_start(0)
+    for l in order:
+        flight[l] = start(l, 0)
+    for s in range(ns):
+        small_finish(s, sf)
+        if s + 1 < ns:
+            sf = small_start(s + 1)
+        else:
+            inv = 1.0 / saccs[ns - 1, 7:8, 6:7]
+            small = saccs[ns - 1] * inv
+            gi_ref[...] = small[0:3]
+            gb_ref[...] = small[3:4]
+            gh_ref[...] = small[4 : 4 + hid]
+            go_ref[...] = small[8:11]
+            for k in range(3):
+                terms_ref[k] = small[7, k]
+                gob_ref[k] = small[7, 3 + k]
+        for l in order:
+            finish(l, s, flight[l], None if s + 1 < ns else inv)
+            flight[l] = start(l, s + 1) if s + 1 < ns else gstart(l, ns - 1)
+    for s in range(ns - 1, -1, -1):
+        for l in order:
+            for c in flight[l]:
+                c.wait()
+            flight[l] = gstart(l, s - 1) if s > 0 else []
+
+def all_reduce(x, n, hid, H, order=None, cid=0):
+    stages = stages_of(n, H)
+    ns = len(stages)
+    kmax = max(r for _, r, _, _ in stages) - 1
+    order = order or tuple(range(hid - 1, -1, -1))
+    vm = pl.BlockSpec(memory_space=pltpu.VMEM)
+    sm = pl.BlockSpec(memory_space=pltpu.SMEM)
+    DMA = pltpu.SemaphoreType.DMA
+    return pl.pallas_call(
+        functools.partial(ar_kernel, n, hid, H, stages, order),
+        out_shape=tuple(jax.ShapeDtypeStruct(k, f32) for k in ((hid, H, H), (3, H), (1, H), (hid, H), (3, H), (3,), (3,))),
+        in_specs=[vm],
+        out_specs=(vm, vm, vm, vm, vm, sm, sm),
+        scratch_shapes=[pltpu.VMEM((hid, r - 1, rows, H), f32) for _, r, rows, _ in stages]
+        + [pltpu.VMEM((hid, rows, H), f32) for _, r, rows, _ in stages]
+        + [pltpu.VMEM((r - 1, 16, H), f32) for _, r, rows, _ in stages]
+        + [pltpu.VMEM((ns, 16, H), f32)]
+        + [DMA((hid, ns, kmax)), DMA((hid, ns, kmax)), DMA((hid, ns, kmax)), DMA((hid, ns, kmax)), DMA((ns, kmax)), DMA((ns, kmax))],
+        compiler_params=pltpu.CompilerParams(collective_id=cid, has_side_effects=True, vmem_limit_bytes=32 * 1024 * 1024),
+        name="all_reduce",
+    )(x)
+
+
+def shards(n, data, counts, offsets, in_w, in_b, w, hb, wo, bo):
     hid, H, _ = w.shape
-    mine = local_terms(counts, offsets, counts_data, in_w, in_b, w, hb, wo, bo)
-    g = lax.psum(mine, "pts")
-    base = hid * H
-    total = g[base + 7, 6]
-    g = g / total
-    return (
-        g[base : base + 3],
-        g[base + 3],
-        g[:base].reshape(hid, H, H),
-        g[base + 4 : base + 4 + hid],
-        g[base + 8 : base + 11],
-        g[base + 7, 3:6],
-        g[base + 7, 0:3],
-    )
+    mine = local_terms(counts, offsets, data, in_w, in_b, w, hb, wo, bo)
+    gw, gi, gb, gh, go, gob, terms = all_reduce(mine, n, hid, H)
+    return gi, gb.reshape(H), gw, gh, go, gob, terms
 
 
 def solution(mesh):
     placed = (P(None, "pts"), P("pts"), P("pts"), P(), P(), P(), P(), P(), P())
     return jax.shard_map(
-        shards,
+        functools.partial(shards, mesh.shape["pts"]),
         mesh=mesh,
         in_specs=placed,
         out_specs=(P(), P(), P(), P(), P(), P(), P()),

time: 179 us -> 61.4 us (0.34)
  waiting for transfers between devices: 137 us -> 0 us
  Pallas kernels: 20.8 us -> 53.8 us
  between operations: 15.3 us -> 1.94 us
  other arithmetic: 1.84 us -> 0 us
    psum x1 -> x0, waiting for transfers between devices: 137 us -> none  [shards(): g = lax.psum(mine, 'pts')]
    pallas_call x0 -> x1, Pallas kernels: none -> 27.2 us  [all_reduce(): pl.pallas_call(functools.partial(ar_kernel, n, hid, H, stages, order), ou...]
    pallas_call x1, Pallas kernels: 20.8 us -> 26.6 us  [local_terms(): pl.pallas_call(functools.partial(local_kernel, H, hid), out_shape=jax.Sha...]
    unnamed x0 -> x9, local copies, waits for them, and re-layouts: none -> 5.38 us
    slice x4 -> x0, local copies, waits for them, and re-layouts: 3.35 us -> none  [the longest x1 1.25 us: shards(): total = g[base + 7, 6]]
    div x1 -> x0, other arithmetic: 1.84 us -> none  [shards(): g = g / total]
  transfers between devices with their start and end apart: 1 -> 0, of which waited for: 1 -> 0; matrix products, arithmetic and copies ran while one was open for 0% -> 0% of each run, Pallas kernels for 0% -> 0%
where the time goes in v1:
time: 61.4 us; the launch traced here: 61.1 us
  Pallas kernels  53.8 us (88%)
  local copies, waits for them, and re-layouts  5.38 us (9%)
  between operations  1.94 us (3%)
    pallas_call x1, Pallas kernels, all_reduce(): pl.pallas_call(functools.partial(ar_kernel, n, hid, H, stages, order), ou...  27.2 us
    pallas_call x1, Pallas kernels, local_terms(): pl.pallas_call(functools.partial(local_kernel, H, hid), out_shape=jax.Sha...  26.6 us
    unnamed x9, local copies, waits for them, and re-layouts  5.38 us

profile of v1, /device:TPU:0, one launch (start us, length us, event | category | flops | bytes accessed | tf_op | source)
XLA Modules:
  0.0 61.1 jit_solution(7966979893416550292)
XLA Ops:
  1.9 26.6 %local_terms.1.x_ref = f32[784,256]{1,0:T(8,128)} custom-call(s32[1]{0:T(128)S(6)} %copy.23.count_ref, s32[1]{0:T(128)S(6)} %copy.24.offset_ref, f32[5,1024]{1,0:T(8,128)} %data_ref.1, f32[3,256]{1,0:T(4,128)} %in_ref.1, f32[1,256]{1,0:T(1,128)} %bitcast.3, f32[3,256,256]{2,1,0:T(8,128)} %w_ref.1, f32[3,256]{1,0:T(4,128)} %hb_ref.1, f32[3,256]{1,0:T(4,128)} %wo_ref.1, ...), custom_call_target="tpu_custom_call" | custom-call | tf_op jit(solution)/shard_map/local_terms/pallas_call | solution.py:235
  28.5 0.0 copy-start
  28.5 1.1 %copy-done = f32[784,256]{1,0:T(8,128)S(1)} copy-done((f32[784,256]{1,0:T(8,128)S(1)}, f32[784,256]{1,0:T(8,128)}, u32[]{:S(2)}) %copy-start) | copy-done | bytes 802840
  29.6 27.2 %all_reduce.1 = (f32[3,256,256]{2,1,0:T(8,128)S(1)}, f32[3,256]{1,0:T(4,128)S(1)}, f32[1,256]{1,0:T(1,128)S(1)}, f32[3,256]{1,0:T(4,128)S(1)}, f32[3,256]{1,0:T(4,128)S(1)}, /*index=5*/f32[3]{0:T(128)S(1)}, f32[3]{0:T(128)S(1)}) custom-call(f32[784,256]{1,0:T(8,128)S(1)} %copy-done), custom_call_target="tpu_custom_call" | custom-call | tf_op jit(solution)/shard_map/all_reduce/pallas_call | solution.py:397
  56.9 0.6 copy.25
  57.5 0.6 copy.26
  58.0 0.9 %copy.27 = f32[3,256,256]{2,1,0:T(8,128)} copy(f32[3,256,256]{2,1,0:T(8,128)S(1)} %get-tuple-element.30) | data formatting | bytes 1572864
  58.9 0.6 copy.28
  59.5 0.6 copy.29
  60.1 0.5 copy.30
  60.6 0.5 copy.31
Async XLA Ops:
  28.5 1.1 %copy-start = (f32[784,256]{1,0:T(8,128)S(1)}, f32[784,256]{1,0:T(8,128)}, u32[]{:S(2)}) copy-start(f32[784,256]{1,0:T(8,128)} %local_terms.1.x_ref) | copy-start | bytes 2408452
